TPU v7x, 32 devices: a whole 2x2x4 slice. The times are simulated.
32 devices in a mesh: row: 4 (over z), col: 8 (over y, x, core).
Axes of the slice: x: 2, y: 2, z: 4, core: 2. Of those that a mesh axis runs over, the one named last changes fastest.
Arguments:
- air_flux: bfloat16 [4, 4096, 16, 128], P(None, ('row', 'col')), may hold values from -1 to 3
- air_area: float32 [4096, 128], P(('row', 'col')), may hold values from 0.2 to 2
- sea_area: float32 [4096, 128], P(('row', 'col')), may hold values from 0.2 to 2
- wet_mask: int32 [4096], P(('row', 'col')), may hold values 0 or 1
- intersection_tiles: bfloat16 [32, 128, 128], replicated, may hold values from -0.125 to 0.125
- send_block: int32 [32, 256], P(('row', 'col')), may hold values from 0 to 127
- target_slot: int32 [4096, 16], P(('row', 'col')), may hold values from 0 to 255
- target_tile: int32 [4096, 16], P(('row', 'col')), may hold values from 0 to 31, as said below
Outputs:
- sea_flux: float32 [4096, 16, 128], P(('row', 'col'))
Inputs may be any that keep to these rules, and one draw needn't show every extreme that they name: `target_tile`: the 16 entries of a row are distinct.
All inputs are finite; a program needn't handle non-finite values. No bound on the sum of `wet_mask` on one device may be relied on, other than what follows from the above.
Results may differ from a plain program's by a relative error of at most 0.0003.
The roundings to bfloat16 on the way count: a program that leaves them out, or rounds other values in their place, can miss the bound.
Values may be sent and summed in bfloat16 or wider, within the bound.
No kernel may reach another device: no remote copies, remote signals or barrier semaphores. Data moves between devices by JAX's collectives and lax.ppermute only.
A program may use at most 128 MiB of HBM per device.

v0:
```python
import jax
import jax.numpy as jnp
from jax import lax
from jax.sharding import PartitionSpec as P

NSTEPS = 4


def regrid_fields(source_rows, row_index, tile_index, intersection_tiles):
    targets = tile_index.shape[0]
    intersections = tile_index.shape[1]
    fields = source_rows.shape[1]
    cell_count = source_rows.shape[2]
    picked = jnp.take(source_rows, row_index.reshape(-1), axis=0).reshape(
        targets, intersections, fields, cell_count
    )
    tile_ids = jnp.arange(intersection_tiles.shape[0], dtype=jnp.int32)
    onehot = (tile_index[:, :, None] == tile_ids[None, None, :]).astype(jnp.bfloat16)
    grouped = jnp.einsum(
        "tkw,tkfc->twfc", onehot, picked, preferred_element_type=jnp.float32
    ).astype(jnp.bfloat16)
    return jnp.einsum(
        "twfc,wcd->tfd", grouped, intersection_tiles, preferred_element_type=jnp.float32
    )


def body(
    air_flux, air_area, sea_area, wet_mask, intersection_tiles, send_block, target_slot, target_tile
):
    mean_flux = jnp.sum(air_flux, axis=0, dtype=jnp.float32) / NSTEPS
    sent_flux = mean_flux.astype(jnp.bfloat16)
    air_part = jnp.sum(mean_flux * air_area[:, None, :], axis=(0, 2))
    air_total = lax.psum(air_part, ("row", "col"))
    outbound = jnp.take(sent_flux, send_block[0], axis=0)
    raw_flux = regrid_fields(
        lax.all_to_all(outbound, "col", split_axis=0, concat_axis=0, tiled=True),
        target_slot,
        target_tile,
        intersection_tiles,
    )
    wet_float = wet_mask.astype(jnp.float32)
    wet_area = wet_float[:, None] * sea_area
    sea_part = jnp.sum(raw_flux * wet_area[:, None, :], axis=(0, 2))
    wet_part = jnp.sum(wet_area)
    sea_total, wet_sum = lax.psum((sea_part, wet_part), ("row", "col"))
    shift = (air_total - sea_total) / jnp.maximum(wet_sum, 1.0)
    return wet_float[:, None, None] * (raw_flux + shift[None, :, None])


def solution(mesh):
    placed = (
        P(None, ("row", "col"), None, None),
        P(("row", "col"), None),
        P(("row", "col"), None),
        P(("row", "col")),
        P(),
        P(("row", "col"), None),
        P(("row", "col"), None),
        P(("row", "col"), None),
    )
    return jax.shard_map(
        body, mesh=mesh, in_specs=placed, out_specs=P(("row", "col"), None, None), check_vma=False
    )
```

profile of v0, /device:TPU:0, one launch (start us, length us, event | category | flops | bytes accessed | tf_op | source)
XLA Modules:
  0.0 115.9 jit_solution(8608368607367261870)
XLA Ops:
  0.0 0.0 copy-start
  0.0 0.0 copy-start.2
  0.0 0.0 copy-start.4
  0.0 0.0 copy-start.3
  0.0 0.0 copy-start.1
  0.0 0.8 compare_select_fusion.2
  0.8 0.7 compare_and_fusion.1
  1.5 0.8 broadcast_multiply_fusion.1
  2.3 2.0 %convert_reduce_fusion = f32[128,16,128]{2,1,0:T(8,128)S(1)} fusion(bf16[4,128,16,128]{3,2,1,0:T(8,128)(2,1)} %param.8), kind=kLoop, calls=%fused_computation.8 | loop fusion | flops 1835008 | bytes 3145728 | tf_op jit(solution)/shard_map/reduce_sum | solution.py:30
  4.4 0.3 multiply_reduce_fusion.1
  4.7 0.9 gather_fusion
  5.5 1.7 %broadcast_select_fusion = bf16[256,16,128]{2,1,0:T(8,128)(2,1)} fusion(bf16[256,16,128]{2,1,0:T(8,128)(2,1)S(1)} %gather_fusion, pred[256]{0:T(512)(128)(4,1)S(1)} %compare_and_fusion.1), kind=kLoop, calls=%fused_computation.16 | loop fusion | flops 524288 | bytes 2097408 | tf_op jit(solution)/shard_map/jit(_take)/select_n | solution.py:34
  7.3 5.2 %all-to-all-start = ((bf16[256,16,128]{2,1,0:T(8,128)(2,1)}), bf16[256,16,128]{2,1,0:T(8,128)(2,1)S(1)}, u32[]{:S(2)}, u32[]{:S(2)}) async-start(bf16[256,16,128]{2,1,0:T(8,128)(2,1)} %broadcast_select_fusion), calls=%async_computation | async-start | bytes 2097152 | tf_op jit(solution)/shard_map/all_to_all | solution.py:36
  12.5 0.0 copy-done.2
  12.5 0.1 copy.18
  12.6 0.0 copy-done.4
  12.6 0.1 copy.17
  12.7 0.0 copy-done.3
  12.7 0.1 copy.16
  12.8 0.1 reshape.80
  13.0 0.0 copy-done.1
  13.0 0.7 fusion.12
  13.7 14.2 %all-to-all-done = bf16[256,16,128]{2,1,0:T(8,128)(2,1)S(1)} async-done(((bf16[256,16,128]{2,1,0:T(8,128)(2,1)}), bf16[256,16,128]{2,1,0:T(8,128)(2,1)S(1)}, u32[]{:S(2)}, u32[]{:S(2)}) %all-to-all-start) | async-done | bytes 1048608 | tf_op jit(solution)/shard_map/all_to_all | solution.py:36
  27.8 16.3 %gather_fusion.1 = bf16[2048,16,128]{2,1,0:T(8,128)(2,1)} fusion(bf16[256,16,128]{2,1,0:T(8,128)(2,1)S(1)} %all-to-all-done, s32[2048]{0:T(1024)S(1)} %broadcast_clamp_fusion), kind=kCustom, calls=%fused_computation.1 | custom fusion | bytes 16785408 | tf_op jit(solution)/shard_map/jit(_take)/gather | solution.py:14
  44.1 12.9 %convolution_convert_fusion = bf16[128,32,16,128]{3,1,2,0:T(8,128)(2,1)} fusion(bf16[128,16,16,128]{3,2,1,0:T(8,128)(2,1)} %bitcast.19, pred[128,16]{1,0:T(8,128)(4,1)S(1)} %copy.17, s32[128,16]{1,0:T(8,128)S(1)} %copy.16), kind=kOutput, calls=%fused_computation.4 | convolution fusion | flops 281083904 | bytes 25176064 | tf_op jit(solution)/shard_map/tkw,tkfc->twfc/dot_general | solution.py:19
  57.0 0.0 copy-done
  57.0 16.8 %multiply_reduce_fusion = (f32[16]{0:T(128)S(1)}, f32[128,16,128]{2,0,1:T(8,128)S(1)}) fusion(f32[128,128]{1,0:T(8,128)S(1)} %get-tuple-element.9, bf16[32,128,128]{2,1,0:T(8,128)(2,1)S(1)} %copy-done, bf16[128,32,16,128]{3,1,2,0:T(8,128)(2,1)} %convolution_convert_fusion), kind=kOutput, calls=%fused_computation.12 | convolution fusion | flops 2148007936 | bytes 18939968 | tf_op jit(solution)/shard_map/twfc,wcd->tfd/dot_general | solution.py:22
  73.8 39.6 %all-reduce = (f32[16]{0:T(128)S(1)}, f32[16]{0:T(128)S(1)}, f32[]{:T(128)}) all-reduce(f32[16]{0:T(128)S(1)} %get-tuple-element.10, f32[16]{0:T(128)S(1)} %get-tuple-element.12, f32[]{:T(128)} %get-tuple-element.8), channel_id=1, replica_groups=mesh['row'=4,'col'=8] {'row','col'}, use_global_device_ids=true, to_apply=%region_2.0 | all-reduce | flops 33 | bytes 264 | tf_op jit(solution)/shard_map/psum | solution.py:33
  114.1 0.2 add_multiply_fusion
  114.3 1.6 %copy.21 = f32[128,16,128]{2,1,0:T(8,128)} copy(f32[128,16,128]{2,0,1:T(8,128)S(1)} %add_multiply_fusion) | data formatting | bytes 2097152 | tf_op jit(solution)/shard_map/mul | solution.py:47
  (6 shorter events, 0.0 us)
Async XLA Ops:
  0.0 57.0 %copy-start = (bf16[32,128,128]{2,1,0:T(8,128)(2,1)S(1)}, bf16[32,128,128]{2,1,0:T(8,128)(2,1)}, u32[]{:S(2)}) copy-start(bf16[32,128,128]{2,1,0:T(8,128)(2,1)} %param.12) | copy-start | bytes 3145732
  0.0 12.5 %copy-start.2 = (s32[128,16]{0,1:T(8,128)S(1)}, s32[128,16]{0,1:T(8,128)}, u32[]{:S(2)}) copy-start(s32[128,16]{0,1:T(8,128)} %param.14) | copy-start | bytes 24580
  0.0 12.6 %copy-start.4 = (s32[128]{0:T(128)S(1)}, s32[128]{0:T(128)}, u32[]{:S(2)}) copy-start(s32[128]{0:T(128)} %param.11) | copy-start | bytes 1540
  0.0 12.7 %copy-start.3 = (s32[128,16]{0,1:T(8,128)S(1)}, s32[128,16]{0,1:T(8,128)}, u32[]{:S(2)}) copy-start(s32[128,16]{0,1:T(8,128)} %param.15) | copy-start | bytes 24580
  0.0 12.9 %copy-start.1 = (f32[128,128]{1,0:T(8,128)S(1)}, f32[128,128]{1,0:T(8,128)}, u32[]{:S(2)}) copy-start(f32[128,128]{1,0:T(8,128)} %param.10) | copy-start | bytes 196612
  7.3 20.6 %all-to-all-start = ((bf16[256,16,128]{2,1,0:T(8,128)(2,1)}), bf16[256,16,128]{2,1,0:T(8,128)(2,1)S(1)}, u32[]{:S(2)}, u32[]{:S(2)}) async-start(bf16[256,16,128]{2,1,0:T(8,128)(2,1)} %broadcast_select_fusion), calls=%async_computation | async-start | bytes 2097152 | tf_op jit(solution)/shard_map/all_to_all | solution.py:36
where the time goes:
time: 116 us
  blocking collectives  39.6 us (34%)
  matrix products  29.7 us (26%)
  local copies, waits for them, and re-layouts  19.1 us (16%)
  waiting for transfers between devices  14.2 us (12%)
  other arithmetic  7.32 us (6%)
  starting transfers between devices  5.2 us (4%)
    psum x1, blocking collectives, body(): air_total = lax.psum(air_part, ('row', 'col'))  39.6 us
    dot_general x1, matrix products, regrid_fields(): jnp.einsum('twfc,wcd->tfd', grouped, intersection_tiles, preferred_elemen...  16.8 us
    gather x1, local copies, waits for them, and re-layouts, regrid_fields(): jnp.take(source_rows, row_index.reshape(-1), axis=0)  16.3 us
    all_to_all x1, waiting for transfers between devices, body(): lax.all_to_all(outbound, 'col', split_axis=0, concat_axis=0, tiled=True)  14.2 us
    dot_general x1, matrix products, regrid_fields(): jnp.einsum('tkw,tkfc->twfc', onehot, picked, preferred_element_type=jnp.f...  12.9 us
    all_to_all x1, starting transfers between devices, body(): lax.all_to_all(outbound, 'col', split_axis=0, concat_axis=0, tiled=True)  5.2 us
    select_n x2, other arithmetic, body(): outbound = jnp.take(sent_flux, send_block[0], axis=0)  2.49 us
  transfers between devices with their start and end apart: 1, of which 1 were waited for; matrix products, arithmetic and copies ran while one was open for 1% of the time, Pallas kernels for 0%

commit v1 on v0

--- a/solution.py
+++ b/solution.py
@@ -30,7 +30,7 @@
     mean_flux = jnp.sum(air_flux, axis=0, dtype=jnp.float32) / NSTEPS
     sent_flux = mean_flux.astype(jnp.bfloat16)
     air_part = jnp.sum(mean_flux * air_area[:, None, :], axis=(0, 2))
-    air_total = lax.psum(air_part, ("row", "col"))
+    air_total = lax.psum(lax.psum(air_part, "col"), "row")
     outbound = jnp.take(sent_flux, send_block[0], axis=0)
     raw_flux = regrid_fields(
         lax.all_to_all(outbound, "col", split_axis=0, concat_axis=0, tiled=True),

time: 116 us -> 134 us (1.16)
  blocking collectives: 39.6 us -> 70.9 us
  waiting for transfers between devices: 14.2 us -> 0.01 us
    psum x1 -> x3, blocking collectives: 39.6 us -> 70.9 us  [the longest x1 37.1 us: body(): sea_total, wet_sum = lax.psum((sea_part, wet_part), ('row', 'col'))]
    all_to_all x1, waiting for transfers between devices: 14.2 us -> 0.01 us  [body(): lax.all_to_all(outbound, 'col', split_axis=0, concat_axis=0, tiled=True)]
  transfers between devices with their start and end apart: 1 -> 1, of which waited for: 1 -> 0; matrix products, arithmetic and copies ran while one was open for 1% -> 1% of each run, Pallas kernels for 0% -> 0%
where the time goes in v1:
time: 134 us; the launch traced here: 133 us
  blocking collectives  70.9 us (53%)
  matrix products  29.7 us (22%)
  local copies, waits for them, and re-layouts  19.1 us (14%)
  other arithmetic  7.32 us (5%)
  starting transfers between devices  5.2 us (4%)
    psum x1, blocking collectives, body(): sea_total, wet_sum = lax.psum((sea_part, wet_part), ('row', 'col'))  37.1 us
    psum x2, blocking collectives, body(): air_total = lax.psum(lax.psum(air_part, 'col'), 'row')  33.8 us
    dot_general x1, matrix products, regrid_fields(): jnp.einsum('twfc,wcd->tfd', grouped, intersection_tiles, preferred_elemen...  16.8 us
    gather x1, local copies, waits for them, and re-layouts, regrid_fields(): jnp.take(source_rows, row_index.reshape(-1), axis=0)  16.3 us
    dot_general x1, matrix products, regrid_fields(): jnp.einsum('tkw,tkfc->twfc', onehot, picked, preferred_element_type=jnp.f...  12.9 us
    all_to_all x1, starting transfers between devices, body(): lax.all_to_all(outbound, 'col', split_axis=0, concat_axis=0, tiled=True)  5.2 us
  transfers between devices with their start and end apart: 1, of which 0 were waited for; matrix products, arithmetic and copies ran while one was open for 1% of the time, Pallas kernels for 0%

profile of v1, /device:TPU:0, one launch (start us, length us, event | category | flops | bytes accessed | tf_op | source)
XLA Modules:
  0.0 133.0 jit_solution(9874883947793075072)
XLA Ops:
  0.0 0.0 copy-start
  0.0 0.0 copy-start.2
  0.0 0.0 copy-start.4
  0.0 0.0 copy-start.3
  0.0 0.0 copy-start.1
  0.0 0.8 compare_select_fusion.2
  0.8 0.7 compare_and_fusion.1
  1.5 0.8 broadcast_multiply_fusion.1
  2.3 2.0 %convert_reduce_fusion = f32[128,16,128]{2,1,0:T(8,128)S(1)} fusion(bf16[4,128,16,128]{3,2,1,0:T(8,128)(2,1)} %param.8), kind=kLoop, calls=%fused_computation.8 | loop fusion | flops 1835008 | bytes 3145728 | tf_op jit(solution)/shard_map/reduce_sum | solution.py:30
  4.4 0.3 multiply_reduce_fusion.1
  4.7 0.9 gather_fusion
  5.5 1.7 %broadcast_select_fusion = bf16[256,16,128]{2,1,0:T(8,128)(2,1)} fusion(bf16[256,16,128]{2,1,0:T(8,128)(2,1)S(1)} %gather_fusion, pred[256]{0:T(512)(128)(4,1)S(1)} %compare_and_fusion.1), kind=kLoop, calls=%fused_computation.16 | loop fusion | flops 524288 | bytes 2097408 | tf_op jit(solution)/shard_map/jit(_take)/select_n | solution.py:34
  7.3 5.2 %all-to-all-start = ((bf16[256,16,128]{2,1,0:T(8,128)(2,1)}), bf16[256,16,128]{2,1,0:T(8,128)(2,1)S(1)}, u32[]{:S(2)}, u32[]{:S(2)}) async-start(bf16[256,16,128]{2,1,0:T(8,128)(2,1)} %broadcast_select_fusion), calls=%async_computation | async-start | bytes 2097152 | tf_op jit(solution)/shard_map/all_to_all | solution.py:36
  12.5 0.0 copy-done.2
  12.5 21.9 %psum.28 = f32[16]{0:T(128)S(1)} all-reduce(f32[16]{0:T(128)S(1)} %get-tuple-element.9), channel_id=1, replica_groups=mesh['row'=4,'col'=8] {'col'}, use_global_device_ids=true, to_apply=%region_2.0 | all-reduce | flops 16 | bytes 128 | tf_op jit(solution)/shard_map/psum | solution.py:33
  34.3 0.1 copy.18
  34.4 0.0 copy-done.4
  34.5 0.1 copy.17
  34.6 0.0 copy-done.3
  34.6 0.1 copy.16
  34.7 0.1 reshape.80
  34.8 12.0 %psum.29 = f32[16]{0:T(128)S(1)} all-reduce(f32[16]{0:T(128)S(1)} %psum.28), channel_id=1, replica_groups=mesh['row'=4,'col'=8] {'row'}, use_global_device_ids=true, to_apply=%region_3.0 | all-reduce | flops 16 | bytes 128 | tf_op jit(solution)/shard_map/psum | solution.py:33
  46.8 0.0 copy-done.1
  46.8 0.7 fusion.12
  47.5 0.0 all-to-all-done
  47.5 16.3 %gather_fusion.1 = bf16[2048,16,128]{2,1,0:T(8,128)(2,1)} fusion(bf16[256,16,128]{2,1,0:T(8,128)(2,1)S(1)} %all-to-all-done, s32[2048]{0:T(1024)S(1)} %broadcast_clamp_fusion), kind=kCustom, calls=%fused_computation.1 | custom fusion | bytes 16785408 | tf_op jit(solution)/shard_map/jit(_take)/gather | solution.py:14
  63.7 12.9 %convolution_convert_fusion = bf16[128,32,16,128]{3,1,2,0:T(8,128)(2,1)} fusion(bf16[128,16,16,128]{3,2,1,0:T(8,128)(2,1)} %bitcast.19, pred[128,16]{1,0:T(8,128)(4,1)S(1)} %copy.17, s32[128,16]{1,0:T(8,128)S(1)} %copy.16), kind=kOutput, calls=%fused_computation.4 | convolution fusion | flops 281083904 | bytes 25176064 | tf_op jit(solution)/shard_map/tkw,tkfc->twfc/dot_general | solution.py:19
  76.7 0.0 copy-done
  76.7 16.8 %multiply_reduce_fusion = (f32[16]{0:T(128)S(1)}, f32[128,16,128]{2,0,1:T(8,128)S(1)}) fusion(f32[128,128]{1,0:T(8,128)S(1)} %get-tuple-element.8, bf16[32,128,128]{2,1,0:T(8,128)(2,1)S(1)} %copy-done, bf16[128,32,16,128]{3,1,2,0:T(8,128)(2,1)} %convolution_convert_fusion), kind=kOutput, calls=%fused_computation.12 | convolution fusion | flops 2148007936 | bytes 18939968 | tf_op jit(solution)/shard_map/twfc,wcd->tfd/dot_general | solution.py:22
  93.5 37.1 %all-reduce = (f32[16]{0:T(128)S(1)}, f32[]{:T(128)}) all-reduce(f32[16]{0:T(128)S(1)} %get-tuple-element.11, f32[]{:T(128)} %get-tuple-element.7), channel_id=1, replica_groups=mesh['row'=4,'col'=8] {'row','col'}, use_global_device_ids=true, to_apply=%region_5.6 | all-reduce | flops 17 | bytes 136 | tf_op jit(solution)/shard_map/psum | solution.py:45
  131.2 0.2 add_multiply_fusion
  131.5 1.6 %copy.21 = f32[128,16,128]{2,1,0:T(8,128)} copy(f32[128,16,128]{2,0,1:T(8,128)S(1)} %add_multiply_fusion) | data formatting | bytes 2097152 | tf_op jit(solution)/shard_map/mul | solution.py:47
  (6 shorter events, 0.0 us)
Async XLA Ops:
  0.0 76.7 %copy-start = (bf16[32,128,128]{2,1,0:T(8,128)(2,1)S(1)}, bf16[32,128,128]{2,1,0:T(8,128)(2,1)}, u32[]{:S(2)}) copy-start(bf16[32,128,128]{2,1,0:T(8,128)(2,1)} %param.12) | copy-start | bytes 3145732
  0.0 12.5 %copy-start.2 = (s32[128,16]{0,1:T(8,128)S(1)}, s32[128,16]{0,1:T(8,128)}, u32[]{:S(2)}) copy-start(s32[128,16]{0,1:T(8,128)} %param.14) | copy-start | bytes 24580
  0.0 34.4 %copy-start.4 = (s32[128]{0:T(128)S(1)}, s32[128]{0:T(128)}, u32[]{:S(2)}) copy-start(s32[128]{0:T(128)} %param.11) | copy-start | bytes 1540
  0.0 34.6 %copy-start.3 = (s32[128,16]{0,1:T(8,128)S(1)}, s32[128,16]{0,1:T(8,128)}, u32[]{:S(2)}) copy-start(s32[128,16]{0,1:T(8,128)} %param.15) | copy-start | bytes 24580
  0.0 46.8 %copy-start.1 = (f32[128,128]{1,0:T(8,128)S(1)}, f32[128,128]{1,0:T(8,128)}, u32[]{:S(2)}) copy-start(f32[128,128]{1,0:T(8,128)} %param.10) | copy-start | bytes 196612
  7.3 40.2 %all-to-all-start = ((bf16[256,16,128]{2,1,0:T(8,128)(2,1)}), bf16[256,16,128]{2,1,0:T(8,128)(2,1)S(1)}, u32[]{:S(2)}, u32[]{:S(2)}) async-start(bf16[256,16,128]{2,1,0:T(8,128)(2,1)} %broadcast_select_fusion), calls=%async_computation | async-start | bytes 2097152 | tf_op jit(solution)/shard_map/all_to_all | solution.py:36
